TPU v7x, 32 devices: a whole 2x2x4 slice. The times are simulated.
32 devices in a mesh: dp: 4 (over y, x), fsdp: 8 (over z, core).
Axes of the slice: x: 2, y: 2, z: 4, core: 2. Of those that a mesh axis runs over, the one named last changes fastest.
Arguments:
- tokens: bfloat16 [32768, 768], P(('dp', 'fsdp')), may hold values from -6 to 6
- segment_ids: int32 [64, 512], P(('dp', 'fsdp')), may hold values from 0 to 7, as said below
- out_grad: bfloat16 [32768, 768], P(('dp', 'fsdp')), may hold values from -6 to 6
- qkv_weight: bfloat16 [768, 2304], P(('dp', 'fsdp')), may hold values from -0.21875 to 0.21875
- query_bias: bfloat16 [768], P(('dp', 'fsdp')), may hold values from -4 to 4
- value_bias: bfloat16 [768], P(('dp', 'fsdp')), may hold values from -4 to 4
- out_weight: bfloat16 [768, 768], P(('dp', 'fsdp')), may hold values from -0.875 to 0.875
- out_bias: bfloat16 [768], P(('dp', 'fsdp')), may hold values from -4 to 4
- attn_gain: bfloat16 [768], P(('dp', 'fsdp')), may hold values from 0.099609375 to 1.8984375
- attn_shift: bfloat16 [768], P(('dp', 'fsdp')), may hold values from -4 to 4
- up_weight: bfloat16 [768, 3072], P(('dp', 'fsdp')), may hold values from -0.21875 to 0.21875
- up_bias: bfloat16 [3072], P(('dp', 'fsdp')), may hold values from -4 to 4
- down_weight: bfloat16 [3072, 768], P(('dp', 'fsdp')), may hold values from -0.109375 to 0.109375
- down_bias: bfloat16 [768], P(('dp', 'fsdp')), may hold values from -4 to 4
- final_gain: bfloat16 [768], P(('dp', 'fsdp')), may hold values from 0.099609375 to 1.8984375
- final_shift: bfloat16 [768], P(('dp', 'fsdp')), may hold values from -4 to 4
Outputs:
- layer_out: bfloat16 [32768, 768], P(('dp', 'fsdp'))
- pooled: float32 [64, 8, 5, 768], P(('dp', 'fsdp'))
- tokens_grad: bfloat16 [32768, 768], P(('dp', 'fsdp'))
- qkv_weight_grad: float32 [768, 2304], P(('dp', 'fsdp'))
- query_bias_grad: float32 [768], P(('dp', 'fsdp'))
- value_bias_grad: float32 [768], P(('dp', 'fsdp'))
- out_weight_grad: float32 [768, 768], P(('dp', 'fsdp'))
- out_bias_grad: float32 [768], P(('dp', 'fsdp'))
- attn_gain_grad: float32 [768], P(('dp', 'fsdp'))
- attn_shift_grad: float32 [768], P(('dp', 'fsdp'))
- up_weight_grad: float32 [768, 3072], P(('dp', 'fsdp'))
- up_bias_grad: float32 [3072], P(('dp', 'fsdp'))
- down_weight_grad: float32 [3072, 768], P(('dp', 'fsdp'))
- down_bias_grad: float32 [768], P(('dp', 'fsdp'))
- final_gain_grad: float32 [768], P(('dp', 'fsdp'))
- final_shift_grad: float32 [768], P(('dp', 'fsdp'))
Inputs may be any that keep to these rules, and one draw needn't show every extreme that they name: `segment_ids`: in every packed row ids start at 0, never fall and rise by at most 1, so a row holds 1 to 8 segments; row 0 holds 8.
All inputs are finite; a program needn't handle non-finite values.
Results may differ from a plain program's by a relative error of at most 0.014.
Values may be sent and summed in bfloat16 or wider, within the bound.
A program may use at most 192 MiB of HBM per device.

v0:
```python
import jax
import jax.numpy as jnp
from jax import lax
from jax.sharding import PartitionSpec as P

D = 768
HEADS = 12
HD = 64
SEGS = 8
NPREF = 5


def layer_norm(values, norm_gain, norm_shift):
    row_mean = jnp.mean(values, axis=-1, keepdims=True)
    centered = values - row_mean
    row_var = jnp.mean(centered * centered, axis=-1, keepdims=True)
    return centered * lax.rsqrt(row_var + 1e-05) * norm_gain + norm_shift


def gelu_exact(values):
    return jax.nn.gelu(values, approximate=False)


def divisor_below(count, limit):
    return max(
        (
            candidate
            for candidate in range(1, count + 1)
            if count % candidate == 0 and candidate <= limit
        )
    )


def masked_scores(queries, key_part, segment_group):
    scores = jnp.einsum(
        "gqhd,gkhd->ghqk", queries, key_part, preferred_element_type=jnp.float32
    ) * HD ** (-0.5)
    allowed = (segment_group[:, :, None] == segment_group[:, None, :])[:, None]
    return jnp.where(allowed, scores, -1000000000.0)


def attend_forward(packed):
    qkv_group, segment_group = packed
    masked = masked_scores(qkv_group[:, :, 0], qkv_group[:, :, 1], segment_group)
    row_top = jnp.max(masked, axis=-1, keepdims=True)
    lifted = jnp.exp(masked - row_top)
    row_total = jnp.sum(lifted, axis=-1, keepdims=True)
    attn_probs = lifted / row_total
    context = jnp.einsum(
        "ghqk,gkhd->gqhd",
        attn_probs.astype(jnp.bfloat16),
        qkv_group[:, :, 2],
        preferred_element_type=jnp.float32,
    ).astype(jnp.bfloat16)
    return (context, row_top + jnp.log(row_total))


def attend_backward(packed):
    qkv_group, segment_group, grad_group, log_total = packed
    queries = qkv_group[:, :, 0]
    key_part = qkv_group[:, :, 1]
    value_part = qkv_group[:, :, 2]
    attn_probs = jnp.exp(masked_scores(queries, key_part, segment_group) - log_total)
    prob_grad = jnp.einsum(
        "gqhd,gkhd->ghqk", grad_group, value_part, preferred_element_type=jnp.float32
    )
    row_dot = jnp.sum(attn_probs * prob_grad, axis=-1, keepdims=True)
    score_grad = (attn_probs * (prob_grad - row_dot)).astype(jnp.bfloat16)
    value_grad = jnp.einsum(
        "ghqk,gqhd->gkhd",
        attn_probs.astype(jnp.bfloat16),
        grad_group,
        preferred_element_type=jnp.float32,
    )
    query_grad = jnp.einsum(
        "ghqk,gkhd->gqhd", score_grad, key_part, preferred_element_type=jnp.float32
    ) * HD ** (-0.5)
    key_grad = jnp.einsum(
        "ghqk,gqhd->gkhd", score_grad, queries, preferred_element_type=jnp.float32
    ) * HD ** (-0.5)
    return jnp.stack([query_grad, key_grad, value_grad], axis=2).astype(jnp.bfloat16)


def pool_rows(outputs, segment_block):
    row_count = segment_block.shape[0]
    length = segment_block.shape[1]
    by_row = outputs.reshape(row_count, length, D)
    member = (segment_block[:, None, :] == jnp.arange(SEGS)[None, :, None]).astype(jnp.float32)
    seg_sums = jnp.einsum("gsl,gld->gsd", member, by_row, precision=lax.Precision.HIGHEST)
    seg_counts = jnp.sum(member, axis=-1, keepdims=True)
    seg_means = seg_sums / jnp.maximum(seg_counts, 1.0)
    columns = jnp.arange(D)
    prefixes = []
    for level in range(NPREF):
        limit = D if level == NPREF - 1 else min(64 * 2**level, D)
        kept_cols = seg_means * (columns < limit).astype(jnp.float32)
        prefixes.append(
            kept_cols * lax.rsqrt(jnp.sum(kept_cols * kept_cols, axis=-1, keepdims=True) + 1e-06)
        )
    return jnp.stack(prefixes, axis=2)


def per_device(
    tokens,
    segment_ids,
    out_grad,
    qkv_weight,
    query_bias,
    value_bias,
    out_weight,
    out_bias,
    attn_gain,
    attn_shift,
    up_weight,
    up_bias,
    down_weight,
    down_bias,
    final_gain,
    final_shift,
):
    attn_full = (
        lax.all_gather(qkv_weight, ("dp", "fsdp"), axis=0, tiled=True),
        lax.all_gather(query_bias, ("dp", "fsdp"), axis=0, tiled=True),
        lax.all_gather(value_bias, ("dp", "fsdp"), axis=0, tiled=True),
        lax.all_gather(out_weight, ("dp", "fsdp"), axis=0, tiled=True),
        lax.all_gather(out_bias, ("dp", "fsdp"), axis=0, tiled=True),
        lax.all_gather(attn_gain, ("dp", "fsdp"), axis=0, tiled=True),
        lax.all_gather(attn_shift, ("dp", "fsdp"), axis=0, tiled=True),
    )
    qkv_full, query_full, value_full, out_full, out_bias_full, attn_gain_full, attn_shift_full = (
        attn_full
    )
    width = out_full.shape[0]
    row_count, length = segment_ids.shape
    per_group = divisor_below(row_count, max(1, 512 // length))
    groups = row_count // per_group
    qkv_bias = jnp.concatenate([query_full, jnp.zeros_like(query_full), value_full]).astype(
        jnp.float32
    )
    qkv = (jnp.dot(tokens, qkv_full, preferred_element_type=jnp.float32) + qkv_bias).astype(
        jnp.bfloat16
    )
    qkv_groups = qkv.reshape(groups, per_group, length, 3, HEADS, HD)
    segment_groups = segment_ids.reshape(groups, per_group, length)
    context, log_total = lax.map(attend_forward, (qkv_groups, segment_groups))
    context = context.reshape(row_count * length, width)
    attn_out = jnp.dot(
        context, out_full, preferred_element_type=jnp.float32
    ) + out_bias_full.astype(jnp.float32)
    resid_one = tokens.astype(jnp.float32) + attn_out
    normed = layer_norm(
        resid_one, attn_gain_full.astype(jnp.float32), attn_shift_full.astype(jnp.float32)
    )
    normed_low = normed.astype(jnp.bfloat16)
    ffn_full = (
        lax.all_gather(up_weight, ("dp", "fsdp"), axis=0, tiled=True),
        lax.all_gather(up_bias, ("dp", "fsdp"), axis=0, tiled=True),
        lax.all_gather(down_weight, ("dp", "fsdp"), axis=0, tiled=True),
        lax.all_gather(down_bias, ("dp", "fsdp"), axis=0, tiled=True),
        lax.all_gather(final_gain, ("dp", "fsdp"), axis=0, tiled=True),
        lax.all_gather(final_shift, ("dp", "fsdp"), axis=0, tiled=True),
    )
    up_full, up_bias_full, down_full, down_bias_full, final_gain_full, final_shift_full = ffn_full
    hidden_pre = jnp.dot(
        normed_low, up_full, preferred_element_type=jnp.float32
    ) + up_bias_full.astype(jnp.float32)
    activated = gelu_exact(hidden_pre).astype(jnp.bfloat16)
    ffn_out = jnp.dot(
        activated, down_full, preferred_element_type=jnp.float32
    ) + down_bias_full.astype(jnp.float32)
    resid_two = normed + ffn_out
    final_out, final_pull = jax.vjp(
        layer_norm,
        resid_two,
        final_gain_full.astype(jnp.float32),
        final_shift_full.astype(jnp.float32),
    )
    pooled = pool_rows(final_out, segment_ids)
    back_up, back_down = (
        lax.all_gather(up_weight, ("dp", "fsdp"), axis=0, tiled=True),
        lax.all_gather(down_weight, ("dp", "fsdp"), axis=0, tiled=True),
    )
    back_qkv, back_out, back_gain = (
        lax.all_gather(qkv_weight, ("dp", "fsdp"), axis=0, tiled=True),
        lax.all_gather(out_weight, ("dp", "fsdp"), axis=0, tiled=True),
        lax.all_gather(attn_gain, ("dp", "fsdp"), axis=0, tiled=True),
    )
    resid_two_grad, final_gain_grad, final_shift_grad = final_pull(out_grad.astype(jnp.float32))
    ffn_grad = resid_two_grad.astype(jnp.bfloat16)
    down_weight_grad = jnp.einsum(
        "tf,td->fd", activated, ffn_grad, preferred_element_type=jnp.float32
    )
    down_bias_grad = jnp.sum(ffn_grad.astype(jnp.float32), axis=0)
    act_grad = jnp.einsum("td,fd->tf", ffn_grad, back_down, preferred_element_type=jnp.float32)
    _, gelu_pull = jax.vjp(gelu_exact, hidden_pre)
    hidden_grad = gelu_pull(act_grad)[0].astype(jnp.bfloat16)
    up_weight_grad = jnp.einsum(
        "td,tf->df", normed_low, hidden_grad, preferred_element_type=jnp.float32
    )
    up_bias_grad = jnp.sum(hidden_grad.astype(jnp.float32), axis=0)
    normed_grad = resid_two_grad + jnp.einsum(
        "tf,df->td", hidden_grad, back_up, preferred_element_type=jnp.float32
    )
    ffn_sums = (
        lax.psum_scatter(up_weight_grad, ("dp", "fsdp"), scatter_dimension=0, tiled=True),
        lax.psum_scatter(up_bias_grad, ("dp", "fsdp"), scatter_dimension=0, tiled=True),
        lax.psum_scatter(down_weight_grad, ("dp", "fsdp"), scatter_dimension=0, tiled=True),
        lax.psum_scatter(down_bias_grad, ("dp", "fsdp"), scatter_dimension=0, tiled=True),
        lax.psum_scatter(final_gain_grad, ("dp", "fsdp"), scatter_dimension=0, tiled=True),
        lax.psum_scatter(final_shift_grad, ("dp", "fsdp"), scatter_dimension=0, tiled=True),
    )
    _, attn_pull = jax.vjp(
        layer_norm, resid_one, back_gain.astype(jnp.float32), attn_shift_full.astype(jnp.float32)
    )
    resid_one_grad, attn_gain_grad, attn_shift_grad = attn_pull(normed_grad)
    attn_grad = resid_one_grad.astype(jnp.bfloat16)
    out_weight_grad = jnp.einsum(
        "td,te->de", context, attn_grad, preferred_element_type=jnp.float32
    )
    out_bias_grad = jnp.sum(attn_grad.astype(jnp.float32), axis=0)
    context_grad = jnp.einsum(
        "te,de->td", attn_grad, back_out, preferred_element_type=jnp.float32
    ).astype(jnp.bfloat16)
    grad_groups = context_grad.reshape(groups, per_group, length, HEADS, HD)
    qkv_grad = lax.map(attend_backward, (qkv_groups, segment_groups, grad_groups, log_total))
    qkv_grad = qkv_grad.reshape(row_count * length, 3 * width)
    qkv_weight_grad = jnp.einsum("td,te->de", tokens, qkv_grad, preferred_element_type=jnp.float32)
    query_bias_grad = jnp.sum(qkv_grad[:, :width].astype(jnp.float32), axis=0)
    value_bias_grad = jnp.sum(qkv_grad[:, 2 * width :].astype(jnp.float32), axis=0)
    tokens_grad = (
        resid_one_grad
        + jnp.einsum("te,de->td", qkv_grad, back_qkv, preferred_element_type=jnp.float32)
    ).astype(jnp.bfloat16)
    attn_sums = (
        lax.psum_scatter(qkv_weight_grad, ("dp", "fsdp"), scatter_dimension=0, tiled=True),
        lax.psum_scatter(query_bias_grad, ("dp", "fsdp"), scatter_dimension=0, tiled=True),
        lax.psum_scatter(value_bias_grad, ("dp", "fsdp"), scatter_dimension=0, tiled=True),
        lax.psum_scatter(out_weight_grad, ("dp", "fsdp"), scatter_dimension=0, tiled=True),
        lax.psum_scatter(out_bias_grad, ("dp", "fsdp"), scatter_dimension=0, tiled=True),
        lax.psum_scatter(attn_gain_grad, ("dp", "fsdp"), scatter_dimension=0, tiled=True),
        lax.psum_scatter(attn_shift_grad, ("dp", "fsdp"), scatter_dimension=0, tiled=True),
    )
    return (
        (final_out.astype(jnp.bfloat16), pooled, tokens_grad) + tuple(attn_sums) + tuple(ffn_sums)
    )


def solution(mesh):
    return jax.shard_map(
        per_device,
        mesh=mesh,
        in_specs=(
            P(("dp", "fsdp"), None),
            P(("dp", "fsdp"), None),
            P(("dp", "fsdp"), None),
            P(("dp", "fsdp"), None),
            P(("dp", "fsdp")),
            P(("dp", "fsdp")),
            P(("dp", "fsdp"), None),
            P(("dp", "fsdp")),
            P(("dp", "fsdp")),
            P(("dp", "fsdp")),
            P(("dp", "fsdp"), None),
            P(("dp", "fsdp")),
            P(("dp", "fsdp"), None),
            P(("dp", "fsdp")),
            P(("dp", "fsdp")),
            P(("dp", "fsdp")),
        ),
        out_specs=(
            P(("dp", "fsdp"), None),
            P(("dp", "fsdp"), None, None, None),
            P(("dp", "fsdp"), None),
            P(("dp", "fsdp"), None),
            P(("dp", "fsdp")),
            P(("dp", "fsdp")),
            P(("dp", "fsdp"), None),
            P(("dp", "fsdp")),
            P(("dp", "fsdp")),
            P(("dp", "fsdp")),
            P(("dp", "fsdp"), None),
            P(("dp", "fsdp")),
            P(("dp", "fsdp"), None),
            P(("dp", "fsdp")),
            P(("dp", "fsdp")),
            P(("dp", "fsdp")),
        ),
        check_vma=False,
    )
```

profile of v0, /device:TPU:0, one launch (start us, length us, event | category | flops | bytes accessed | tf_op | source)
XLA Modules:
  0.0 834.6 jit_solution(5160416906497867386)
XLA Ops:
  18.3 42.6 %all-reduce.19 = (bf16[768]{0:T(1024)(128)(2,1)S(1)}, bf16[768]{0:T(1024)(128)(2,1)S(1)}, bf16[768]{0:T(1024)(128)(2,1)S(1)}, bf16[768]{0:T(1024)(128)(2,1)S(1)}...) all-reduce(bf16[768]{0:T(1024)(128)(2,1)S(1)} %dynamic-update-slice, ...), channel_id=1, replica_groups=mesh['dp'=4,'fsdp'=8] {'dp','fsdp'}, use_global_device_ids=true, to_apply=%add.1 | all-reduce | flops 9216 | bytes 36864
  64.5 9.4 %all-gather.5.cloned.1.call-done = bf16[768,2304]{1,0:T(8,128)(2,1)} async-done(((bf16[24,2304]{1,0:T(8,128)(2,1)}), bf16[768,2304]{1,0:T(8,128)(2,1)}) %all-gather.5.cloned.1.call-update) | async-done | bytes 3538960 | tf_op jit(solution)/shard_map/all_gather | solution.py:122
  73.9 8.5 %add_convert_fusion.1 = bf16[1024,2304]{1,0:T(8,128)(2,1)} fusion(bf16[1024,768]{1,0:T(8,128)(2,1)} %param.20, bf16[768,2304]{1,0:T(8,128)(2,1)} %all-gather.5.cloned.1.call-done, f32[2304]{0:T(1024)S(1)} %maximum_convert_fusion), kind=kOutput, calls=%fused_computation.67 | convolution fusion | flops 3628597248 | bytes 9839616 | tf_op jit(solution)/shard_map/dot_general | solution.py:140
  82.3 6.6 copy.58
  89.0 8.9 %reshape.465 = bf16[2,1,512,3,12,64]{2,0,5,4,3,1:T(2,128)(2,1)} reshape(bf16[1024,2304]{0,1:T(8,128)(2,1)} %copy.58) | data formatting | bytes 9437184 | tf_op jit(solution)/shard_map/reshape | solution.py:143
  97.9 5.6 copy.59
  103.4 22.5 %while.22 = (s32[]{:T(128)}, bf16[2,1,512,12,64]{2,4,3,1,0:T(8,128)(2,1)}, f32[2,1,12,512,1]{3,2,4,1,0:T(8,128)S(1)}, bf16[2,1,512,3,12,64]{2,5,4,3,1,0:T(8,128)(2,1)}, s32[2,1,512]{2,1,0:T(1,128)S(1)}, /*index=5*/s32[]{:T(128)}) while((s32[]{:T(128)}, bf16[2,1,512,12,64]{2,4,3,1,0:T(8,128)(2,1)}, f32[2,1,12,512,1]{3,2,4,1,0:T(8,128)S(1)}, ...), condition=%wide.region_3.4_spmd, body=%wide.region_0.3_spmd.sunk | while | flops 843704320 | bytes 46905436 | solution.py:145
  103.6 1.8 dynamic-slice_bitcast_fusion.6
  105.5 2.1 fusion.98
  107.6 2.6 fusion.99
  110.2 4.4 fusion.100
  114.8 1.8 dynamic-slice_bitcast_fusion.6
  116.6 2.1 fusion.98
  118.7 2.6 fusion.99
  121.3 4.4 fusion.100
  125.9 3.1 copy.60
  129.0 1.6 copy.73
  130.6 3.9 fusion.58
  135.0 60.5 %all-gather.9.cloned.1.call-done = bf16[768,3072]{1,0:T(8,128)(2,1)} async-done(((bf16[24,3072]{1,0:T(8,128)(2,1)}), bf16[768,3072]{1,0:T(8,128)(2,1)}) %all-gather.9.cloned.1.call-update) | async-done | bytes 4718608 | tf_op jit(solution)/shard_map/all_gather | solution.py:156
  195.5 35.8 %multiply_convert_fusion.3 = (bf16[1024,3072]{1,0:T(8,128)(2,1)}, f32[1024,3072]{1,0:T(8,128)}, f32[1024,3072]{1,0:T(8,128)}) fusion(f32[3072]{0:T(1024)S(1)} %copy-done.29, bf16[768,3072]{1,0:T(8,128)(2,1)} %all-gather.9.cloned.1.call-done, f32[1024,768]{1,0:T(8,128)S(1)} %get-tuple-element.232, f32[768]{0:T(1024)S(1)} %copy-done.18, ...), kind=kOutput, calls=%fused_computation.53 | convolution fusion | flops 5043388416 | bytes 39348224 | tf_op jit(solution)/shard_map/dot_general | solution.py:164
  231.3 29.0 %all-gather.11.cloned.1.call-done = bf16[3072,768]{1,0:T(8,128)(2,1)} async-done(((bf16[96,768]{1,0:T(8,128)(2,1)}), bf16[3072,768]{1,0:T(8,128)(2,1)}) %all-gather.11.cloned.1.call-update) | async-done | bytes 4718608 | tf_op jit(solution)/shard_map/all_gather | solution.py:158
  260.3 9.3 %fusion.59 = (f32[1024]{0:T(1024)S(1)}, f32[1024,768]{1,0:T(8,128)S(1)}) fusion(f32[768]{0:T(1024)S(1)} %copy-done.31, bf16[1024,3072]{1,0:T(8,128)(2,1)} %get-tuple-element.223, bf16[3072,768]{1,0:T(8,128)(2,1)} %all-gather.11.cloned.1.call-done, f32[768]{0:T(1024)S(1)} %copy-done.18, f32[768]{0:T(1024)S(1)} %copy-done.16, f32[1024]{0:T(1024)S(1)} %fusion.48, ...), kind=kOutput, calls=%fused_computation.143 | convolution fusion | flops 4837342208 | bytes 17323008 | tf_op jit(solution)/shard_map/dot_general | solution.py:168
  270.2 1.8 fusion.40
  272.0 3.1 fusion.55
  275.2 2.1 convert_reduce_fusion.2
  277.3 19.0 %convert_reduce_fusion = (f32[3072]{0:T(1024)}, bf16[1024,3072]{1,0:T(8,128)(2,1)}) fusion(f32[1024,3072]{1,0:T(8,128)} %get-tuple-element.224, bf16[1024,768]{1,0:T(8,128)(2,1)} %get-tuple-element.214, bf16[3072,768]{1,0:T(8,128)(2,1)} %all-gather.11.cloned.1.call-done, f32[1024,3072]{1,0:T(8,128)} %get-tuple-element.233, f32[3072]{0:T(1024)S(1)} %copy-done.29), kind=kOutput, calls=%fused_computation.51 | convolution fusion | flops 4885312512 | bytes 37773312 | tf_op jit(solution)/shard_map/td,fd->tf/dot_general | solution.py:194
  296.2 10.1 %multiply_reduce_fusion.1 = (f32[768]{0:T(1024)}, f32[1024]{0:T(1024)S(1)}, f32[768]{0:T(1024)}, f32[1024,768]{1,0:T(8,128)S(1)}) fusion(f32[1024,768]{1,0:T(8,128)S(1)} %get-tuple-element.232, f32[1024]{0:T(1024)S(1)} %fusion.48, f32[1024]{0:T(1024)S(1)} %broadcast_multiply_fusion.1, f32[768]{0:T(1024)S(1)} %copy-done.16, ...), kind=kOutput, calls=%fused_computation.79 | convolution fusion | flops 4839699456 | bytes 20472832 | tf_op jit(solution)/shard_map/tf,df->td/dot_general | solution.py:201
  306.4 1.6 fusion.54
  308.1 1.6 copy-done.3
  310.6 2.8 fusion.60
  313.4 2.7 convolution_convert_fusion
  316.9 2.4 reshape.469
  319.3 1.7 copy.63
  321.1 52.3 %while.23 = (s32[]{:T(128)}, bf16[2,1,512,3,12,64]{2,5,4,3,1,0:T(8,128)(2,1)}, bf16[2,1,512,3,12,64]{2,5,4,3,1,0:T(8,128)(2,1)}, s32[2,1,512]{2,1,0:T(1,128)S(1)...) while((s32[]{:T(128)}, ...), condition=%wide.region_20.21_spmd, body=%wide.region_18.20_spmd.sunk | while | flops 2069751808 | bytes 112916592 | solution.py:225
  321.4 1.8 dynamic-slice_bitcast_fusion.7
  323.2 1.8 fusion.105
  325.0 3.1 fusion.106
  328.2 7.2 multiply_reduce_fusion.11
  335.3 7.1 multiply_convert_fusion.5
  343.6 2.0 fusion.107
  345.6 1.6 maximum_dynamic-update-slice_fusion.2
  347.4 1.9 dynamic-slice_bitcast_fusion.7
  349.3 1.8 fusion.105
  351.1 3.1 fusion.106
  354.3 7.2 multiply_reduce_fusion.11
  361.4 7.0 multiply_convert_fusion.5
  369.6 2.0 fusion.107
  371.6 1.7 maximum_dynamic-update-slice_fusion.2
  373.4 9.4 %copy.64 = bf16[2,1,512,3,12,64]{2,0,5,4,3,1:T(2,128)(2,1)} copy(bf16[2,1,512,3,12,64]{2,5,4,3,1,0:T(8,128)(2,1)} %get-tuple-element.78) | data formatting | bytes 9437184 | tf_op jit(solution)/shard_map/while | solution.py:225
  382.8 4.0 copy.74
  386.8 2.1 copy-done.2
  388.9 5.8 convolution_bitcast_fusion
  394.8 8.0 copy.71
  402.9 1.8 copy-done.1
  404.7 10.7 %fusion.50 = f32[768,3072]{1,0:T(8,128)} fusion(bf16[1024,3072]{1,0:T(8,128)(2,1)} %get-tuple-element.239, f32[1024,768]{1,0:T(8,128)S(1)} %copy-done.1, f32[768]{0:T(1024)S(1)} %copy-done.19, f32[768]{0:T(1024)S(1)} %copy-done.17, f32[1024]{0:T(1024)S(1)} %copy-done.13, f32[1024]{0:T(1024)S(1)} %copy-done.11), kind=kOutput, calls=%fused_computation.137 | convolution fusion | flops 4835770368 | bytes 18888704 | tf_op jit(solution)/shard_map/td,tf->df/dot_general | solution.py:197
  415.5 1.3 copy-done.7
  416.8 10.4 %fusion.61 = f32[3072,768]{1,0:T(8,128)} fusion(bf16[1024,3072]{1,0:T(8,128)(2,1)} %get-tuple-element.223, bf16[1024,768]{1,0:T(8,128)(2,1)S(1)} %copy-done.7), kind=kOutput, calls=%fused_computation.145 | convolution fusion | flops 4831838208 | bytes 17301504 | tf_op jit(solution)/shard_map/tf,td->fd/dot_general | solution.py:190
  428.1 3.5 multiply_reduce_fusion.5
  432.7 2.5 convert_reduce_fusion.4
  435.2 39.8 %all-reduce.18 = (f32[768]{0:T(1024)S(1)}, f32[768]{0:T(1024)S(1)}, f32[768]{0:T(1024)S(1)}, f32[768]{0:T(1024)S(1)}, f32[768]{0:T(1024)S(1)}, /*index=5*/f32[30...) all-reduce(f32[768]{0:T(1024)S(1)} %get-tuple-element.165, ...), channel_id=3, replica_groups=mesh['dp'=4,'fsdp'=8] {'dp','fsdp'}, use_global_device_ids=true, to_apply=%region_23.24.clone | all-reduce | flops 9216 | bytes 73728
  480.3 8.6 %add_convert_fusion.2 = bf16[1024,768]{1,0:T(8,128)(2,1)} fusion(f32[1024,768]{1,0:T(8,128)S(1)} %copy-done.4, bf16[1024,2304]{0,1:T(8,128)(2,1)} %bitcast.169, bf16[768,2304]{1,0:T(8,128)(2,1)} %all-gather.5.cloned.1.call-done, f32[1024]{0:T(1024)S(1)} %copy-done.23), kind=kOutput, calls=%fused_computation.83 | convolution fusion | flops 3626237952 | bytes 12980224 | tf_op jit(solution)/shard_map/te,de->td/dot_general | solution.py:232
  488.9 54.9 %reduce-scatter.13.cloned.1.call-done = f32[24,2304]{1,0:T(8,128)} async-done(((f32[768,2304]{1,0:T(8,128)}), f32[24,2304]{1,0:T(8,128)}) %reduce-scatter.13.cloned.1.call-update) | async-done | bytes 221200
  543.9 141.9 %reduce-scatter.9.cloned.1.call-done = f32[24,3072]{1,0:T(8,128)} async-done(((f32[768,3072]{1,0:T(8,128)}), f32[24,3072]{1,0:T(8,128)}) %reduce-scatter.9.cloned.1.call-update) | async-done | bytes 294928 | tf_op jit(solution)/shard_map/reduce_scatter | solution.py:205
  685.7 141.6 %reduce-scatter.11.cloned.1.call-done = f32[96,768]{1,0:T(8,128)} async-done(((f32[3072,768]{1,0:T(8,128)}), f32[96,768]{1,0:T(8,128)}) %reduce-scatter.11.cloned.1.call-update) | async-done | bytes 294928 | tf_op jit(solution)/shard_map/reduce_scatter | solution.py:207
  (166 shorter events, 27.8 us)
Async XLA Ops:
  7.2 66.7 %all-gather.5.cloned.1.call-start = ((), (), s32[]{:S(2)}) async-start(), calls=%async_computation.4 | async-start | bytes 3649536 | tf_op jit(solution)/shard_map/all_gather | solution.py:122
  7.9 122.7 %all-gather.7.cloned.1.call-start = ((), (), s32[]{:S(2)}) async-start(), calls=%async_computation.5 | async-start | bytes 1216512 | tf_op jit(solution)/shard_map/all_gather | solution.py:125
  8.7 186.8 %all-gather.9.cloned.1.call-start = ((), (), s32[]{:S(2)}) async-start(), calls=%async_computation.6 | async-start | bytes 4866048 | tf_op jit(solution)/shard_map/all_gather | solution.py:156
  9.4 250.9 %all-gather.11.cloned.1.call-start = ((), (), s32[]{:S(2)}) async-start(), calls=%async_computation.7 | async-start | bytes 4866048 | tf_op jit(solution)/shard_map/all_gather | solution.py:158
  10.0 479.0 %reduce-scatter.7.cloned.1.call-start = ((), (), s32[]{:S(2)}) async-start(), calls=%async_computation.8 | async-start | bytes 2433024 | tf_op jit(solution)/shard_map/reduce_scatter | solution.py:238
  125.9 4.7 copy-start.8
  125.9 4.7 copy-start.14
  130.6 64.9 %copy-start.16 = (f32[768]{0:T(1024)S(1)}, f32[768]{0:T(1024)}, u32[]{:S(2)}) copy-start(f32[768]{0:T(1024)} %convert_element_type.150) | copy-start | bytes 9220
  130.6 64.9 %copy-start.18 = (f32[768]{0:T(1024)S(1)}, f32[768]{0:T(1024)}, u32[]{:S(2)}) copy-start(f32[768]{0:T(1024)} %convert_element_type.151) | copy-start | bytes 9220
  130.6 64.9 %copy-start.29 = (f32[3072]{0:T(1024)S(1)}, f32[3072]{0:T(1024)}, u32[]{:S(2)}) copy-start(f32[3072]{0:T(1024)} %convert_element_type.153) | copy-start | bytes 36868
  134.5 171.9 %copy-start = (f32[1024,768]{1,0:T(8,128)}, f32[1024,768]{1,0:T(8,128)S(1)}, u32[]{:S(2)}) copy-start(f32[1024,768]{1,0:T(8,128)S(1)} %get-tuple-element.232) | copy-start | bytes 9437188
  134.5 171.9 %copy-start.10 = (f32[1024]{0:T(1024)}, f32[1024]{0:T(1024)S(1)}, u32[]{:S(2)}) copy-start(f32[1024]{0:T(1024)S(1)} %broadcast_multiply_fusion.1) | copy-start | bytes 12292
  135.0 171.4 %copy-start.12 = (f32[1024]{0:T(1024)}, f32[1024]{0:T(1024)S(1)}, u32[]{:S(2)}) copy-start(f32[1024]{0:T(1024)S(1)} %fusion.48) | copy-start | bytes 12292
  135.0 125.3 %copy-start.31 = (f32[768]{0:T(1024)S(1)}, f32[768]{0:T(1024)}, u32[]{:S(2)}) copy-start(f32[768]{0:T(1024)} %convert_element_type.155) | copy-start | bytes 9220
  260.3 9.9 %copy-start.5 = (bf16[1024,768]{1,0:T(8,128)(2,1)S(1)}, bf16[1024,768]{1,0:T(8,128)(2,1)}, u32[]{:S(2)}) copy-start(bf16[1024,768]{1,0:T(8,128)(2,1)} %param.22) | copy-start | bytes 4718596
  260.3 9.9 %copy-start.20 = (f32[768]{0:T(1024)S(1)}, f32[768]{0:T(1024)}, u32[]{:S(2)}) copy-start(f32[768]{0:T(1024)} %convert_element_type.156) | copy-start | bytes 9220
  269.6 2.4 copy-start.24
  308.0 1.7 copy-start.3
  308.0 2.6 copy-start.6
  308.1 2.6 copy-start.22
  316.9 4.2 copy-start.9
  316.9 4.2 copy-start.15
  321.0 222.8 %reduce-scatter.13.cloned.1.call-start = ((), (), s32[]{:S(2)}) async-start(), calls=%async_computation.11 | async-start | bytes 7299072
  382.8 6.1 copy-start.34
  386.8 2.1 copy-start.2
  402.8 1.9 copy-start.1
  402.8 1.9 copy-start.11
  402.8 1.9 copy-start.13
  402.8 1.9 copy-start.17
  402.8 1.9 copy-start.19
  402.9 282.9 %reduce-scatter.9.cloned.1.call-start = ((), (), s32[]{:S(2)}) async-start(), calls=%async_computation.9 | async-start | bytes 9732096 | tf_op jit(solution)/shard_map/reduce_scatter | solution.py:205
  415.4 1.4 copy-start.7
  415.5 411.9 %reduce-scatter.11.cloned.1.call-start = ((), (), s32[]{:S(2)}) async-start(), calls=%async_computation.10 | async-start | bytes 9732096 | tf_op jit(solution)/shard_map/reduce_scatter | solution.py:207
  427.3 0.7 copy-start.21
  427.3 7.9 copy-start.25
  427.3 7.9 copy-start.26
  427.3 7.9 copy-start.27
  427.3 7.9 copy-start.28
  427.4 7.9 copy-start.30
  427.4 7.9 copy-start.32
  427.4 7.9 copy-start.33
  427.4 52.9 %copy-start.4 = (f32[1024,768]{1,0:T(8,128)S(1)}, f32[1024,768]{1,0:T(8,128)}, u32[]{:S(2)}) copy-start(f32[1024,768]{1,0:T(8,128)} %copy-done.3) | copy-start | bytes 9437188
  427.4 52.9 %copy-start.23 = (f32[1024]{0:T(1024)S(1)}, f32[1024]{0:T(1024)}, u32[]{:S(2)}) copy-start(f32[1024]{0:T(1024)} %copy-done.22) | copy-start | bytes 12292
Sparse Core Ops, SparseCore 0:
  11.0 62.8 all-gather.4
  76.9 52.9 all-gather.6
  132.9 62.4 all-gather.8
  198.3 61.9 all-gather.10
  321.1 97.8 reduce-scatter.6
  425.2 118.6 reduce-scatter.12
  550.3 135.3 reduce-scatter.8
  692.2 135.1 reduce-scatter.10
where the time goes:
time: 846 us; the launch traced here: 835 us
  waiting for transfers between devices  440 us (52%)
  matrix products  175 us (21%)
  blocking collectives  82.4 us (10%)
  local copies, waits for them, and re-layouts  81 us (10%)
  other arithmetic  40.5 us (5%)
  between operations  15.2 us (2%)
    reduce_scatter x1, waiting for transfers between devices, per_device(): lax.psum_scatter(up_weight_grad, ('dp', 'fsdp'), scatter_dimension=0, til...  142 us
    reduce_scatter x1, waiting for transfers between devices, per_device(): lax.psum_scatter(down_weight_grad, ('dp', 'fsdp'), scatter_dimension=0, t...  142 us
    unnamed x2, blocking collectives  82.4 us
    all_gather x1, waiting for transfers between devices, per_device(): lax.all_gather(up_weight, ('dp', 'fsdp'), axis=0, tiled=True)  60.5 us
    unnamed x9, waiting for transfers between devices  57.6 us
    dot_general x1, matrix products, per_device(): jnp.dot(normed_low, up_full, preferred_element_type=jnp.float32)  35.8 us
    unnamed x102, local copies, waits for them, and re-layouts  34.6 us
    all_gather x1, waiting for transfers between devices, per_device(): lax.all_gather(down_weight, ('dp', 'fsdp'), axis=0, tiled=True)  29 us
  transfers between devices with their start and end apart: 8, of which 6 were waited for; matrix products, arithmetic and copies ran while one was open for 28% of the time, Pallas kernels for 0%

commit v1 on v0

--- a/solution.py
+++ b/solution.py
@@ -1,7 +1,311 @@
+import functools
+
 import jax
 import jax.numpy as jnp
 from jax import lax
+from jax.experimental import pallas as pl
+from jax.experimental.pallas import tpu as pltpu
 from jax.sharding import PartitionSpec as P
+
+MESH = pl.DeviceIdType.MESH
+BF = jnp.bfloat16
+F32 = jnp.float32
+
+def place():
+    dp = lax.axis_index("dp")
+    fs = lax.axis_index("fsdp")
+    return dp, dp // 2, dp % 2, fs // 2, fs % 2
+
+
+def barrier_all(peers):
+    sem = pltpu.get_barrier_semaphore()
+    for peer in peers:
+        pl.semaphore_signal(sem, inc=1, device_id=peer, device_id_type=MESH)
+    pl.semaphore_wait(sem, len(peers))
+
+
+class Gather:
+    SLOTS = 31
+
+    def __init__(self, srcs, outs, send, recv, local):
+        self.srcs, self.outs, self.send, self.recv, self.local = srcs, outs, send, recv, local
+        dp, y, x, z, c = place()
+        self.dp, self.z, self.c = dp, z, c
+        self.dpx = y * 2 + (1 - x)
+        self.dpy = (1 - y) * 2 + x
+        self.dpd = (1 - y) * 2 + (1 - x)
+        self.me = self.fs(z)
+
+    def fs(self, z):
+        return z * 2 + self.c
+
+    def zk(self, k):
+        return (self.z + 4 - k) % 4
+
+    def peers(self):
+        return [(self.dp, self.fs((self.z + k) % 4)) for k in (1, 2, 3)] + [
+            (self.dpx, self.me), (self.dpy, self.me), (self.dp, self.z * 2 + 1 - self.c)]
+
+    def copy(self, g, dp, z, slot, peer, own=False, n=None):
+        index = dp * 8 + self.fs(z)
+        src = self.srcs[g] if own else self.outs[g].at[index]
+        return pltpu.make_async_remote_copy(
+            src_ref=src, dst_ref=self.outs[g].at[index], send_sem=self.send.at[g, slot],
+            recv_sem=self.recv.at[g, slot], device_id=peer, device_id_type=MESH)
+
+    def msgs(self, g):
+        x, y, core = (self.dpx, self.me), (self.dpy, self.me), (self.dp, self.z * 2 + 1 - self.c)
+        out = {}
+        for k in (1, 2, 3):
+            out[k - 1] = (self.dp, self.z, (self.dp, self.fs((self.z + k) % 4)), True)
+        for k in range(4):
+            out[3 + k] = (self.dp, self.zk(k), x, k == 0)
+            out[7 + k] = (self.dp, self.zk(k), y, k == 0)
+            if k < 2:
+                out[11 + k] = (self.dpy, self.zk(k), x, False)
+            else:
+                out[11 + k] = (self.dpx, self.zk(k), y, False)
+            out[15 + k] = (self.dp, self.zk(k), core, k == 0)
+            out[19 + k] = (self.dpx, self.zk(k), core, False)
+            out[23 + k] = (self.dpy, self.zk(k), core, False)
+            out[27 + k] = (self.dpd, self.zk(k), core, False)
+        return out
+
+    def go(self, g, slot):
+        dp, z, peer, own = self.msgs(g)[slot]
+        self.copy(g, dp, z, slot, peer, own).start()
+
+    def arrived(self, g, slot):
+        dp, z, peer, own = self.msgs(g)[slot]
+        self.copy(g, dp, z, slot, peer, own).wait_recv()
+
+    def start(self, g):
+        pltpu.make_async_copy(self.srcs[g], self.outs[g].at[self.dp * 8 + self.me], self.local.at[g]).start()
+        for slot in (0, 1, 2, 3, 7, 15):
+            self.go(g, slot)
+
+    def step_z(self, g, k):
+        self.arrived(g, k - 1)
+        for slot in (3 + k, 7 + k, 15 + k):
+            self.go(g, slot)
+
+    def step_xy(self, g, k):
+        self.arrived(g, 3 + k)
+        if k >= 2:
+            self.go(g, 11 + k)
+        self.go(g, 19 + k)
+        self.arrived(g, 7 + k)
+        if k < 2:
+            self.go(g, 11 + k)
+        self.go(g, 23 + k)
+
+    def step_d(self, g, k):
+        self.arrived(g, 11 + k)
+        self.go(g, 27 + k)
+
+    def step_core(self, g):
+        for slot in range(15, 31):
+            self.arrived(g, slot)
+
+    def drain(self, g):
+        pltpu.make_async_copy(self.srcs[g], self.outs[g].at[self.dp * 8 + self.me], self.local.at[g]).wait()
+        for slot, (dp, z, peer, own) in self.msgs(g).items():
+            self.copy(g, dp, z, slot, peer, own).wait_send()
+
+
+def gather_kernel(count, *refs):
+    srcs, outs = refs[:count], refs[count:2 * count]
+    send, recv, local = refs[2 * count:]
+    ag = Gather(srcs, outs, send, recv, local)
+    barrier_all(ag.peers())
+    for g in range(count):
+        ag.start(g)
+    for k in (1, 2, 3):
+        for g in range(count):
+            ag.step_z(g, k)
+    for k in range(4):
+        for g in range(count):
+            ag.step_xy(g, k)
+    for k in range(4):
+        for g in range(count):
+            ag.step_d(g, k)
+    for g in range(count):
+        ag.step_core(g)
+    for g in range(count):
+        ag.drain(g)
+
+
+def gather(arrays, cid=0):
+    count = len(arrays)
+    return pl.pallas_call(
+        functools.partial(gather_kernel, count),
+        out_shape=[jax.ShapeDtypeStruct((32,) + a.shape, a.dtype) for a in arrays],
+        in_specs=[pl.BlockSpec(memory_space=pltpu.VMEM)] * count,
+        out_specs=[pl.BlockSpec(memory_space=pl.ANY)] * count,
+        scratch_shapes=[pltpu.SemaphoreType.DMA((count, 31)), pltpu.SemaphoreType.DMA((count, 31)),
+                        pltpu.SemaphoreType.DMA((count,))],
+        compiler_params=pltpu.CompilerParams(collective_id=cid, has_side_effects=True),
+    )(*arrays)
+
+
+class Scatter:
+    SLOTS = 31
+
+    def __init__(self, grads, outs, rc, rd, rxy, rz, sb, keep, send, recv):
+        self.grads, self.outs = grads, outs
+        self.rc, self.rd, self.rxy, self.rz, self.sb, self.keep = rc, rd, rxy, rz, sb, keep
+        self.send, self.recv = send, recv
+        dp, y, x, z, c = place()
+        self.dp, self.z, self.c = dp, z, c
+        self.cols = (dp, y * 2 + (1 - x), (1 - y) * 2 + x, (1 - y) * 2 + (1 - x))
+        self.me = z * 2 + c
+
+    def zk(self, k):
+        return (self.z + 4 - k) % 4
+
+    def peers(self):
+        return [(self.dp, self.zk(k) * 2 + self.c) for k in (1, 2, 3)] + [
+            (self.cols[1], self.me), (self.cols[2], self.me), (self.dp, self.z * 2 + 1 - self.c)]
+
+    def copy(self, g, slot):
+        if slot < 16:
+            p, k = divmod(slot, 4)
+            index = self.cols[p] * 8 + self.zk(k) * 2 + 1 - self.c
+            src, dst, peer = self.grads[g].at[index], self.rc[g].at[slot], (self.dp, self.z * 2 + 1 - self.c)
+        elif slot < 20:
+            k = slot - 16
+            src, dst = self.sb[g].at[12 + k], self.rd[g].at[k]
+            peer = (self.cols[1 if k < 2 else 2], self.me)
+        elif slot < 28:
+            src, dst = self.sb[g].at[slot - 16], self.rxy[g].at[slot - 20]
+            peer = (self.cols[1 if slot < 24 else 2], self.me)
+        else:
+            k = slot - 27
+            src, dst, peer = self.sb[g].at[k], self.rz[g].at[k - 1], (self.dp, self.zk(k) * 2 + self.c)
+        return pltpu.make_async_remote_copy(
+            src_ref=src, dst_ref=dst, send_sem=self.send.at[g, slot], recv_sem=self.recv.at[g, slot],
+            device_id=peer, device_id_type=MESH)
+
+    def start(self, g):
+        for slot in range(12, 16):
+            self.copy(g, slot).start()
+        for slot in range(4, 12):
+            self.copy(g, slot).start()
+        for slot in range(0, 4):
+            self.copy(g, slot).start()
+
+    def add(self, g, slot, terms, dst, dtype):
+        p, k = divmod(slot, 4)
+        index = self.cols[p] * 8 + self.zk(k) * 2 + self.c
+        rows, cols = self.grads[g].shape[1:]
+        step = 32 if rows % 32 == 0 else rows
+        wide = min(cols, 768)
+
+        def part(i, carry):
+            at = (pl.ds(0, rows), pl.ds(pl.multiple_of(i * wide, 128), wide)) if step == rows else (
+                pl.ds(pl.multiple_of(i * step, step), step), pl.ds(0, cols))
+            total = self.grads[g][(index,) + at].astype(F32)
+            for ref, j in terms:
+                total += ref[(j,) + at].astype(F32)
+            if dst is self.outs[g]:
+                dst[at] = total
+            elif dst is self.keep[g]:
+                dst[at] = total
+            else:
+                dst[(slot,) + at] = total.astype(dtype)
+            return carry
+
+        lax.fori_loop(0, cols // wide if step == rows else rows // step, part, 0)
+
+    def step_d(self, g, k):
+        self.copy(g, 12 + k).wait_recv()
+        self.add(g, 12 + k, [(self.rc[g], 12 + k)], self.sb[g], self.sb[g].dtype)
+        self.copy(g, 16 + k).start()
+
+    def step_near(self, g, p, k):
+        slot = p * 4 + k
+        self.copy(g, slot).wait_recv()
+        terms = [(self.rc[g], slot)]
+        if (p == 2) == (k < 2):
+            self.copy(g, 16 + k).wait_recv()
+            terms.append((self.rd[g], k))
+        self.add(g, slot, terms, self.sb[g], self.sb[g].dtype)
+        self.copy(g, 16 + slot).start()
+
+    def step_own(self, g, k):
+        for slot in (k, 20 + k, 24 + k):
+            self.copy(g, slot).wait_recv()
+        terms = [(self.rc[g], k), (self.rxy[g], k), (self.rxy[g], 4 + k)]
+        if k:
+            self.add(g, k, terms, self.sb[g], self.sb[g].dtype)
+            self.copy(g, 27 + k).start()
+        else:
+            self.add(g, k, terms, self.keep[g], F32)
+
+    def finish(self, g):
+        for slot in (28, 29, 30):
+            self.copy(g, slot).wait_recv()
+        rows, cols = self.grads[g].shape[1:]
+        step = 32 if rows % 32 == 0 else rows
+        wide = min(cols, 768)
+
+        def part(i, carry):
+            at = (pl.ds(0, rows), pl.ds(pl.multiple_of(i * wide, 128), wide)) if step == rows else (
+                pl.ds(pl.multiple_of(i * step, step), step), pl.ds(0, cols))
+            total = self.keep[g][at]
+            for k in range(3):
+                total += self.rz[g][(k,) + at].astype(F32)
+            self.outs[g][at] = total
+            return carry
+
+        lax.fori_loop(0, cols // wide if step == rows else rows // step, part, 0)
+
+    def drain(self, g):
+        for slot in range(31):
+            self.copy(g, slot).wait_send()
+
+
+def scatter_scratch(shapes):
+    def bufs(n):
+        return [pltpu.VMEM((n, r, c), t) for (r, c, t) in shapes]
+    return bufs(16) + bufs(4) + bufs(8) + bufs(3) + bufs(12 + 4) + [pltpu.VMEM((r, c), F32) for (r, c, t) in shapes] + [
+        pltpu.SemaphoreType.DMA((len(shapes), 31)), pltpu.SemaphoreType.DMA((len(shapes), 31))]
+
+
+def scatter_kernel(count, *refs):
+    groups = [refs[i * count:(i + 1) * count] for i in range(8)]
+    send, recv = refs[8 * count:]
+    rs = Scatter(*groups, send, recv)
+    barrier_all(rs.peers())
+    for g in range(count):
+        rs.start(g)
+    for k in range(4):
+        for g in range(count):
+            rs.step_d(g, k)
+    for p, k in ((1, 0), (1, 1), (2, 2), (2, 3), (2, 0), (2, 1), (1, 2), (1, 3)):
+        for g in range(count):
+            rs.step_near(g, p, k)
+    for k in (1, 2, 3, 0):
+        for g in range(count):
+            rs.step_own(g, k)
+    for g in range(count):
+        rs.finish(g)
+    for g in range(count):
+        rs.drain(g)
+
+
+def scatter(arrays, cid=1):
+    count = len(arrays)
+    shapes = [a.shape[1:] + (a.dtype,) for a in arrays]
+    return pl.pallas_call(
+        functools.partial(scatter_kernel, count),
+        out_shape=[jax.ShapeDtypeStruct(a.shape[1:], F32) for a in arrays],
+        in_specs=[pl.BlockSpec(memory_space=pltpu.VMEM)] * count,
+        out_specs=[pl.BlockSpec(memory_space=pltpu.VMEM)] * count,
+        scratch_shapes=scatter_scratch(shapes),
+        compiler_params=pltpu.CompilerParams(collective_id=cid, has_side_effects=True, vmem_limit_bytes=60 * 2**20),
+    )(*arrays)
+
 
 D = 768
 HEADS = 12
@@ -99,8 +403,38 @@
         )
     return jnp.stack(prefixes, axis=2)
 
+AXES = ("dp", "fsdp")
+
+
+def gather_all(kernels, weights, vectors, wide):
+    if not kernels:
+        return [lax.all_gather(a, AXES, axis=0, tiled=True) for a in (*weights, *vectors, wide)]
+    part = vectors[0].shape[0]
+    small = jnp.concatenate([*vectors, wide])
+    small = jnp.pad(small, (0, 2048 - small.shape[0])).reshape(16, 128)
+    outs = gather((*weights, small))
+    full = [a.reshape(-1, a.shape[-1]) for a in outs[:-1]]
+    flat = outs[-1].reshape(32, 2048)
+    rows = flat[:, :len(vectors) * part].reshape(32, len(vectors), part).transpose(1, 0, 2).reshape(len(vectors), -1)
+    wide_full = flat[:, len(vectors) * part:len(vectors) * part + wide.shape[0]].reshape(-1)
+    return [*full, *rows, wide_full]
+
+
+def scatter_all(kernels, grads, vectors, wide):
+    if not kernels:
+        return [lax.psum_scatter(a.astype(F32), AXES, scatter_dimension=0, tiled=True) for a in (*grads, *vectors, wide)]
+    part = vectors[0].shape[0] // 32
+    small = jnp.stack(vectors).reshape(len(vectors), 32, part).transpose(1, 0, 2).reshape(32, -1)
+    small = jnp.concatenate([small, wide.reshape(32, -1)], axis=1)
+    small = jnp.pad(small, ((0, 0), (0, 1024 - small.shape[1]))).reshape(32, 8, 128)
+    outs = scatter([a.astype(BF).reshape(32, -1, a.shape[-1]) for a in grads] + [small])
+    flat = outs[-1].reshape(-1)
+    n = len(vectors) * part
+    return [*outs[:-1], *[flat[i * part:(i + 1) * part] for i in range(len(vectors))], flat[n:n + wide.shape[0] // 32]]
+
 
 def per_device(
+    kernels,
     tokens,
     segment_ids,
     out_grad,
@@ -118,18 +452,10 @@
     final_gain,
     final_shift,
 ):
-    attn_full = (
-        lax.all_gather(qkv_weight, ("dp", "fsdp"), axis=0, tiled=True),
-        lax.all_gather(query_bias, ("dp", "fsdp"), axis=0, tiled=True),
-        lax.all_gather(value_bias, ("dp", "fsdp"), axis=0, tiled=True),
-        lax.all_gather(out_weight, ("dp", "fsdp"), axis=0, tiled=True),
-        lax.all_gather(out_bias, ("dp", "fsdp"), axis=0, tiled=True),
-        lax.all_gather(attn_gain, ("dp", "fsdp"), axis=0, tiled=True),
-        lax.all_gather(attn_shift, ("dp", "fsdp"), axis=0, tiled=True),
-    )
-    qkv_full, query_full, value_full, out_full, out_bias_full, attn_gain_full, attn_shift_full = (
-        attn_full
-    )
+    (qkv_full, out_full, up_full, down_full, query_full, value_full, out_bias_full, attn_gain_full,
+     attn_shift_full, down_bias_full, final_gain_full, final_shift_full, up_bias_full) = gather_all(
+        kernels, (qkv_weight, out_weight, up_weight, down_weight),
+        (query_bias, value_bias, out_bias, attn_gain, attn_shift, down_bias, final_gain, final_shift), up_bias)
     width = out_full.shape[0]
     row_count, length = segment_ids.shape
     per_group = divisor_below(row_count, max(1, 512 // length))
@@ -152,15 +478,6 @@
         resid_one, attn_gain_full.astype(jnp.float32), attn_shift_full.astype(jnp.float32)
     )
     normed_low = normed.astype(jnp.bfloat16)
-    ffn_full = (
-        lax.all_gather(up_weight, ("dp", "fsdp"), axis=0, tiled=True),
-        lax.all_gather(up_bias, ("dp", "fsdp"), axis=0, tiled=True),
-        lax.all_gather(down_weight, ("dp", "fsdp"), axis=0, tiled=True),
-        lax.all_gather(down_bias, ("dp", "fsdp"), axis=0, tiled=True),
-        lax.all_gather(final_gain, ("dp", "fsdp"), axis=0, tiled=True),
-        lax.all_gather(final_shift, ("dp", "fsdp"), axis=0, tiled=True),
-    )
-    up_full, up_bias_full, down_full, down_bias_full, final_gain_full, final_shift_full = ffn_full
     hidden_pre = jnp.dot(
         normed_low, up_full, preferred_element_type=jnp.float32
     ) + up_bias_full.astype(jnp.float32)
@@ -176,22 +493,13 @@
         final_shift_full.astype(jnp.float32),
     )
     pooled = pool_rows(final_out, segment_ids)
-    back_up, back_down = (
-        lax.all_gather(up_weight, ("dp", "fsdp"), axis=0, tiled=True),
-        lax.all_gather(down_weight, ("dp", "fsdp"), axis=0, tiled=True),
-    )
-    back_qkv, back_out, back_gain = (
-        lax.all_gather(qkv_weight, ("dp", "fsdp"), axis=0, tiled=True),
-        lax.all_gather(out_weight, ("dp", "fsdp"), axis=0, tiled=True),
-        lax.all_gather(attn_gain, ("dp", "fsdp"), axis=0, tiled=True),
-    )
     resid_two_grad, final_gain_grad, final_shift_grad = final_pull(out_grad.astype(jnp.float32))
     ffn_grad = resid_two_grad.astype(jnp.bfloat16)
     down_weight_grad = jnp.einsum(
         "tf,td->fd", activated, ffn_grad, preferred_element_type=jnp.float32
     )
     down_bias_grad = jnp.sum(ffn_grad.astype(jnp.float32), axis=0)
-    act_grad = jnp.einsum("td,fd->tf", ffn_grad, back_down, preferred_element_type=jnp.float32)
+    act_grad = jnp.einsum("td,fd->tf", ffn_grad, down_full, preferred_element_type=jnp.float32)
     _, gelu_pull = jax.vjp(gelu_exact, hidden_pre)
     hidden_grad = gelu_pull(act_grad)[0].astype(jnp.bfloat16)
     up_weight_grad = jnp.einsum(
@@ -199,18 +507,10 @@
     )
     up_bias_grad = jnp.sum(hidden_grad.astype(jnp.float32), axis=0)
     normed_grad = resid_two_grad + jnp.einsum(
-        "tf,df->td", hidden_grad, back_up, preferred_element_type=jnp.float32
-    )
-    ffn_sums = (
-        lax.psum_scatter(up_weight_grad, ("dp", "fsdp"), scatter_dimension=0, tiled=True),
-        lax.psum_scatter(up_bias_grad, ("dp", "fsdp"), scatter_dimension=0, tiled=True),
-        lax.psum_scatter(down_weight_grad, ("dp", "fsdp"), scatter_dimension=0, tiled=True),
-        lax.psum_scatter(down_bias_grad, ("dp", "fsdp"), scatter_dimension=0, tiled=True),
-        lax.psum_scatter(final_gain_grad, ("dp", "fsdp"), scatter_dimension=0, tiled=True),
-        lax.psum_scatter(final_shift_grad, ("dp", "fsdp"), scatter_dimension=0, tiled=True),
+        "tf,df->td", hidden_grad, up_full, preferred_element_type=jnp.float32
     )
     _, attn_pull = jax.vjp(
-        layer_norm, resid_one, back_gain.astype(jnp.float32), attn_shift_full.astype(jnp.float32)
+        layer_norm, resid_one, attn_gain_full.astype(jnp.float32), attn_shift_full.astype(jnp.float32)
     )
     resid_one_grad, attn_gain_grad, attn_shift_grad = attn_pull(normed_grad)
     attn_grad = resid_one_grad.astype(jnp.bfloat16)
@@ -219,7 +519,7 @@
     )
     out_bias_grad = jnp.sum(attn_grad.astype(jnp.float32), axis=0)
     context_grad = jnp.einsum(
-        "te,de->td", attn_grad, back_out, preferred_element_type=jnp.float32
+        "te,de->td", attn_grad, out_full, preferred_element_type=jnp.float32
     ).astype(jnp.bfloat16)
     grad_groups = context_grad.reshape(groups, per_group, length, HEADS, HD)
     qkv_grad = lax.map(attend_backward, (qkv_groups, segment_groups, grad_groups, log_total))
@@ -229,25 +529,23 @@
     value_bias_grad = jnp.sum(qkv_grad[:, 2 * width :].astype(jnp.float32), axis=0)
     tokens_grad = (
         resid_one_grad
-        + jnp.einsum("te,de->td", qkv_grad, back_qkv, preferred_element_type=jnp.float32)
+        + jnp.einsum("te,de->td", qkv_grad, qkv_full, preferred_element_type=jnp.float32)
     ).astype(jnp.bfloat16)
-    attn_sums = (
-        lax.psum_scatter(qkv_weight_grad, ("dp", "fsdp"), scatter_dimension=0, tiled=True),
-        lax.psum_scatter(query_bias_grad, ("dp", "fsdp"), scatter_dimension=0, tiled=True),
-        lax.psum_scatter(value_bias_grad, ("dp", "fsdp"), scatter_dimension=0, tiled=True),
-        lax.psum_scatter(out_weight_grad, ("dp", "fsdp"), scatter_dimension=0, tiled=True),
-        lax.psum_scatter(out_bias_grad, ("dp", "fsdp"), scatter_dimension=0, tiled=True),
-        lax.psum_scatter(attn_gain_grad, ("dp", "fsdp"), scatter_dimension=0, tiled=True),
-        lax.psum_scatter(attn_shift_grad, ("dp", "fsdp"), scatter_dimension=0, tiled=True),
-    )
+    sums = scatter_all(
+        kernels, (qkv_weight_grad, out_weight_grad, up_weight_grad, down_weight_grad),
+        (query_bias_grad, value_bias_grad, out_bias_grad, attn_gain_grad, attn_shift_grad, down_bias_grad,
+         final_gain_grad, final_shift_grad), up_bias_grad)
+    gq, go, gu, gd, gqb, gvb, gob, gag, gas, gdb, gfg, gfs, gub = sums
     return (
-        (final_out.astype(jnp.bfloat16), pooled, tokens_grad) + tuple(attn_sums) + tuple(ffn_sums)
+        final_out.astype(jnp.bfloat16), pooled, tokens_grad,
+        gq, gqb, gvb, go, gob, gag, gas, gu, gub, gd, gdb, gfg, gfs,
     )
 
 
 def solution(mesh):
+    kernels = dict(mesh.shape) == {"dp": 4, "fsdp": 8}
     return jax.shard_map(
-        per_device,
+        functools.partial(per_device, kernels),
         mesh=mesh,
         in_specs=(
             P(("dp", "fsdp"), None),

time: 846 us -> 484 us (0.57)
  waiting for transfers between devices: 440 us -> 0 us
  Pallas kernels: 0 us -> 207 us
  blocking collectives: 82.4 us -> 0 us
  matrix products: 175 us -> 156 us
  between operations: 15.2 us -> 1.85 us
    reduce_scatter x3 -> x0, waiting for transfers between devices: 283 us -> none  [the longest x1 142 us: per_device(): lax.psum_scatter(up_weight_grad, ('dp', 'fsdp'), scatter_dimension=0, til...]
    pallas_call x0 -> x2, Pallas kernels: none -> 207 us  [the longest x1 124 us: scatter(): pl.pallas_call(functools.partial(scatter_kernel, count), out_shape=[jax.S...]
    all_gather x4 -> x0, waiting for transfers between devices: 98.9 us -> none  [the longest x1 60.5 us: per_device(): lax.all_gather(up_weight, ('dp', 'fsdp'), axis=0, tiled=True)]
    unnamed x2 -> x0, blocking collectives: 82.4 us -> none
    unnamed x9 -> x0, waiting for transfers between devices: 57.6 us -> none
    unnamed x102 -> x110, local copies, waits for them, and re-layouts: 34.6 us -> 15.8 us
  transfers between devices with their start and end apart: 8 -> 0, of which waited for: 6 -> 0; matrix products, arithmetic and copies ran while one was open for 28% -> 0% of each run, Pallas kernels for 0% -> 0%
where the time goes in v1:
time: 484 us; the launch traced here: 478 us
  Pallas kernels  207 us (43%)
  matrix products  156 us (32%)
  local copies, waits for them, and re-layouts  75.3 us (16%)
  other arithmetic  36.9 us (8%)
    pallas_call x1, Pallas kernels, scatter(): pl.pallas_call(functools.partial(scatter_kernel, count), out_shape=[jax.S...  124 us
    pallas_call x1, Pallas kernels, gather(): pl.pallas_call(functools.partial(gather_kernel, count), out_shape=[jax.Sh...  82.4 us
    dot_general x1, matrix products, per_device(): jnp.dot(normed_low, up_full, preferred_element_type=jnp.float32)  35.2 us
    dot_general x1, matrix products, per_device(): jnp.einsum('td,fd->tf', ffn_grad, down_full, preferred_element_type=jnp.f...  16.8 us
    unnamed x110, local copies, waits for them, and re-layouts  15.8 us
    dot_general x2, matrix products, attend_backward(): jnp.einsum('gqhd,gkhd->ghqk', grad_group, value_part, preferred_element_t...  14.3 us
    convert_element_type x2, other arithmetic, attend_backward(): score_grad = (attn_probs * (prob_grad - row_dot)).astype(jnp.bfloat16)  14 us
    while x2, local copies, waits for them, and re-layouts, per_device(): lax.map(attend_backward, (qkv_groups, segment_groups, grad_groups, log_to...  11.1 us

profile of v1, /device:TPU:0, one launch (start us, length us, event | category | flops | bytes accessed | tf_op | source)
XLA Modules:
  0.0 477.6 jit_solution(15875635768803127584)
XLA Ops:
  0.7 6.1 %concatenate.28 = bf16[288]{0:T(512)(128)(2,1)S(1)} concatenate(bf16[24]{0:T(256)(128)(2,1)} %param.24, bf16[24]{0:T(256)(128)(2,1)} %param.25, bf16[24]{0:T(256)(128)(2,1)} %param.27, bf16[24]{0:T(256)(128)(2,1)} %param.28, bf16[24]{0:T(256)(128)(2,1)} %param.29, bf16[24]{0:T(256)(128)(2,1)} %param.33, bf16[24]{0:T(256)(128)(2,1)} %param.34, bf16[24]{0:T(256)(128)(2,1)} %param.35, ...), dimensions={0} | concatenate | bytes 1152 | tf_op jit(solution)/shard_map/concatenate | solution.py:413
  6.8 0.8 convert_reduce_fusion.6
  12.3 82.4 %shard_map.279 = (bf16[32,24,2304]{2,1,0:T(8,128)(2,1)}, bf16[32,24,768]{2,1,0:T(8,128)(2,1)}, bf16[32,24,3072]{2,1,0:T(8,128)(2,1)}, bf16[32,96,768]{2,1,0:T(8,128)(2,1)}, bf16[32,16,128]{2,1,0:T(8,128)(2,1)}) custom-call(bf16[24,2304]{1,0:T(8,128)(2,1)} %refs_0_.1, bf16[24,768]{1,0:T(8,128)(2,1)} %refs_1_.1, bf16[24,3072]{1,0:T(8,128)(2,1)} %refs_2_.1, ...), custom_call_target="tpu_custom_call" | custom-call | tf_op jit(solution)/shard_map/pallas_call | solution.py:140
  94.8 0.9 copy.61
  100.7 9.1 %fusion.37 = bf16[1024,2304]{0,1:T(8,128)(2,1)} fusion(bf16[768,2304]{1,0:T(8,128)(2,1)} %bitcast.218, bf16[1024,768]{1,0:T(8,128)(2,1)} %param.20, f32[2304]{0:T(1024)S(1)} %maximum_convert_fusion), kind=kOutput, calls=%fused_computation.71 | convolution fusion | flops 3628597248 | bytes 9839616 | tf_op jit(solution)/shard_map/dot_general | solution.py:466
  109.8 9.3 %reshape.593 = bf16[2,1,512,3,12,64]{2,0,5,4,3,1:T(2,128)(2,1)} reshape(bf16[1024,2304]{0,1:T(8,128)(2,1)} %fusion.37) | data formatting | bytes 9437184 | tf_op jit(solution)/shard_map/reshape | solution.py:469
  119.1 5.6 %copy.44 = bf16[2,1,512,3,12,64]{2,5,4,3,1,0:T(8,128)(2,1)} copy(bf16[2,1,512,3,12,64]{2,0,5,4,3,1:T(2,128)(2,1)} %reshape.593) | data formatting | bytes 9437184 | tf_op jit(solution)/shard_map/while | solution.py:471
  124.7 22.4 %while.22 = (s32[]{:T(128)}, bf16[2,1,512,12,64]{2,4,3,1,0:T(8,128)(2,1)}, f32[2,1,12,512,1]{3,2,4,1,0:T(8,128)S(1)}, bf16[2,1,512,3,12,64]{2,5,4,3,1,0:T(8,128)(2,1)}, s32[2,1,512]{2,1,0:T(1,128)S(1)}, /*index=5*/s32[]{:T(128)}) while((s32[]{:T(128)}, bf16[2,1,512,12,64]{2,4,3,1,0:T(8,128)(2,1)}, f32[2,1,12,512,1]{3,2,4,1,0:T(8,128)S(1)}, ...), condition=%wide.region_3.4_spmd, body=%wide.region_0.3_spmd.sunk | while | flops 843704320 | bytes 46905436 | solution.py:471
  125.0 1.8 dynamic-slice_bitcast_fusion.6
  126.8 2.1 fusion.104
  128.9 2.6 fusion.105
  131.5 4.4 fusion.106
  136.1 1.8 dynamic-slice_bitcast_fusion.6
  137.9 2.1 fusion.104
  140.1 2.6 fusion.105
  142.6 4.4 fusion.106
  147.2 3.2 copy.45
  150.9 1.7 fusion.66
  153.8 35.2 %multiply_convert_fusion.3 = (bf16[1024,3072]{1,0:T(8,128)(2,1)S(1)}, f32[1024,3072]{1,0:T(8,128)}, f32[1024,3072]{1,0:T(8,128)}) fusion(f32[3072]{0:T(1024)S(1)} %copy-done.32, bf16[768,3072]{1,0:T(8,128)(2,1)S(1)} %bitcast.213, f32[1024,768]{1,0:T(8,128)S(1)} %get-tuple-element.223, f32[768]{0:T(1024)S(1)} %copy-done.34, f32[768]{0:T(1024)S(1)} %copy-done.28, ...), kind=kOutput, calls=%fused_computation.53 | convolution fusion | flops 5043388416 | bytes 39348224 | tf_op jit(solution)/shard_map/dot_general | solution.py:481
  189.2 5.4 %fusion.67 = (f32[1024]{0:T(1024)S(1)}, f32[1024,768]{1,0:T(8,128)S(1)}) fusion(f32[768]{0:T(1024)S(1)} %copy-done.35, bf16[1024,3072]{1,0:T(8,128)(2,1)S(1)} %get-tuple-element.206, bf16[3072,768]{1,0:T(8,128)(2,1)S(1)} %bitcast.217, f32[768]{0:T(1024)S(1)} %copy-done.34, f32[768]{0:T(1024)S(1)} %copy-done.28, f32[1024]{0:T(1024)S(1)} %fusion.56, ...), kind=kOutput, calls=%fused_computation.175 | convolution fusion | flops 4837342208 | bytes 17323008 | tf_op jit(solution)/shard_map/dot_general | solution.py:485
  195.2 1.2 fusion.41
  197.8 3.6 fusion.62
  201.5 1.2 multiply_reduce_fusion.5
  203.2 0.7 copy.51
  204.2 16.8 %convert_reduce_fusion = (f32[3072]{0:T(1024)S(1)}, bf16[1024,3072]{1,0:T(8,128)(2,1)}) fusion(f32[1024,3072]{1,0:T(8,128)} %get-tuple-element.207, bf16[1024,768]{1,0:T(8,128)(2,1)S(1)} %get-tuple-element.197, bf16[3072,768]{1,0:T(8,128)(2,1)} %bitcast.214, f32[1024,3072]{1,0:T(8,128)} %get-tuple-element.224, f32[3072]{0:T(1024)S(1)} %copy-done.32), kind=kOutput, calls=%fused_computation.51 | convolution fusion | flops 4885312512 | bytes 37773312 | tf_op jit(solution)/shard_map/td,fd->tf/dot_general | solution.py:502
  221.0 10.4 %convolution_convert_fusion = bf16[3072,768]{1,0:T(8,128)(2,1)} fusion(bf16[1024,3072]{1,0:T(8,128)(2,1)} %copy-done.42, bf16[1024,768]{1,0:T(8,128)(2,1)S(1)} %get-tuple-element.197), kind=kOutput, calls=%fused_computation.68 | convolution fusion | flops 4834197504 | bytes 12582912 | tf_op jit(solution)/shard_map/tf,td->fd/dot_general | solution.py:498
  231.4 8.4 %multiply_reduce_fusion.1 = (f32[768]{0:T(1024)S(1)}, f32[1024]{0:T(1024)S(1)}, f32[768]{0:T(1024)S(1)}, f32[1024,768]{1,0:T(8,128)S(1)}) fusion(f32[1024,768]{1,0:T(8,128)S(1)} %copy-done.1, f32[1024]{0:T(1024)S(1)} %fusion.56, f32[1024]{0:T(1024)S(1)} %broadcast_multiply_fusion.1, f32[768]{0:T(1024)S(1)} %copy-done.28, ...), kind=kOutput, calls=%fused_computation.82 | convolution fusion | flops 4839699456 | bytes 20472832 | tf_op jit(solution)/shard_map/tf,df->td/dot_general | solution.py:509
  239.8 1.5 fusion.61
  241.3 8.2 %convolution_convert_fusion.1 = bf16[768,3072]{1,0:T(8,128)(2,1)} fusion(bf16[1024,3072]{1,0:T(8,128)(2,1)S(1)} %copy-done.41, f32[1024,768]{1,0:T(8,128)S(1)} %copy-done.1, f32[768]{0:T(1024)S(1)} %copy-done.34, f32[768]{0:T(1024)S(1)} %copy-done.28, f32[1024]{0:T(1024)S(1)} %fusion.56, f32[1024]{0:T(1024)S(1)} %broadcast_multiply_fusion.1), kind=kOutput, calls=%fused_computation.69 | convolution fusion | flops 4838129664 | bytes 14170112 | tf_op jit(solution)/shard_map/td,tf->df/dot_general | solution.py:505
  252.6 1.3 copy-done.6
  254.0 2.4 convolution_convert_fusion.4
  256.4 0.7 stack.65
  257.1 2.8 convolution_convert_fusion.3
  259.9 0.8 copy.46
  260.7 2.4 reshape.600
  263.1 1.7 copy.48
  264.8 52.2 %while.23 = (s32[]{:T(128)}, bf16[2,1,512,3,12,64]{2,5,4,3,1,0:T(8,128)(2,1)}, bf16[2,1,512,3,12,64]{2,5,4,3,1,0:T(8,128)(2,1)}, s32[2,1,512]{2,1,0:T(1,128)S(1)...) while((s32[]{:T(128)}, ...), condition=%wide.region_20.21_spmd, body=%wide.region_18.20_spmd.sunk | while | flops 2069751808 | bytes 112916592 | solution.py:525
  265.1 1.8 dynamic-slice_bitcast_fusion.7
  266.9 1.8 fusion.111
  268.8 3.1 fusion.112
  271.9 7.2 %multiply_reduce_fusion.11 = (f32[12,512]{1,0:T(8,128)S(1)}, f32[12,512,512]{1,2,0:T(8,128)}) fusion(f32[12,512,512]{1,2,0:T(8,128)S(1)} %fusion.111, f32[12,512]{1,0:T(8,128)S(1)} %dynamic-slice_bitcast_fusion.8, pred[512,512]{0,1:T(8,128)(4,1)S(1)} %broadcast_compare_fusion.5, bf16[1,512,3,12,64]{1,4,3,2,0:T(8,128)(2,1)S(1)} %dynamic-slice_bitcast_fusion.7, ...), kind=kOutput, calls=%fused_computation.20.clone.1 | convolution fusion | flops 418375680 | bytes 27058180 | tf_op jit(solution)/shard_map/while/body/eval_jaxpr/gqhd,gkhd->ghqk/dot_general | solution.py:368
  279.1 7.0 %multiply_convert_fusion.5 = bf16[12,512,512]{1,2,0:T(8,128)(2,1)S(1)} fusion(f32[12,512,512]{1,2,0:T(8,128)} %get-tuple-element.309, f32[12,512,512]{1,2,0:T(8,128)S(1)} %fusion.111, f32[12,512]{1,0:T(8,128)S(1)} %get-tuple-element.310, f32[12,512]{1,0:T(8,128)S(1)} %dynamic-slice_bitcast_fusion.8, pred[512,512]{0,1:T(8,128)(4,1)S(1)} %broadcast_compare_fusion.5), kind=kLoop, calls=%fused_computation.19.clone.1 | loop fusion | flops 18874368 | bytes 31768576 | tf_op jit(solution)/shard_map/while/body/eval_jaxpr/convert_element_type | solution.py:372
  286.1 1.1 fusion.114
  287.2 2.0 fusion.113
  289.2 1.6 maximum_dynamic-update-slice_fusion.2
  291.0 1.8 dynamic-slice_bitcast_fusion.7
  292.9 1.8 fusion.111
  294.7 3.1 fusion.112
  297.9 7.2 %multiply_reduce_fusion.11 = (f32[12,512]{1,0:T(8,128)S(1)}, f32[12,512,512]{1,2,0:T(8,128)}) fusion(f32[12,512,512]{1,2,0:T(8,128)S(1)} %fusion.111, f32[12,512]{1,0:T(8,128)S(1)} %dynamic-slice_bitcast_fusion.8, pred[512,512]{0,1:T(8,128)(4,1)S(1)} %broadcast_compare_fusion.5, bf16[1,512,3,12,64]{1,4,3,2,0:T(8,128)(2,1)S(1)} %dynamic-slice_bitcast_fusion.7, ...), kind=kOutput, calls=%fused_computation.20.clone.1 | convolution fusion | flops 418375680 | bytes 27058180 | tf_op jit(solution)/shard_map/while/body/eval_jaxpr/gqhd,gkhd->ghqk/dot_general | solution.py:368
  305.0 7.0 %multiply_convert_fusion.5 = bf16[12,512,512]{1,2,0:T(8,128)(2,1)S(1)} fusion(f32[12,512,512]{1,2,0:T(8,128)} %get-tuple-element.309, f32[12,512,512]{1,2,0:T(8,128)S(1)} %fusion.111, f32[12,512]{1,0:T(8,128)S(1)} %get-tuple-element.310, f32[12,512]{1,0:T(8,128)S(1)} %dynamic-slice_bitcast_fusion.8, pred[512,512]{0,1:T(8,128)(4,1)S(1)} %broadcast_compare_fusion.5), kind=kLoop, calls=%fused_computation.19.clone.1 | loop fusion | flops 18874368 | bytes 31768576 | tf_op jit(solution)/shard_map/while/body/eval_jaxpr/convert_element_type | solution.py:372
  312.0 1.1 fusion.114
  313.1 2.0 fusion.113
  315.1 1.7 maximum_dynamic-update-slice_fusion.2
  317.0 9.4 %copy.49 = bf16[2,1,512,3,12,64]{2,0,5,4,3,1:T(2,128)(2,1)} copy(bf16[2,1,512,3,12,64]{2,5,4,3,1,0:T(8,128)(2,1)} %get-tuple-element.93) | data formatting | bytes 9437184 | tf_op jit(solution)/shard_map/while | solution.py:525
  326.4 4.1 copy.58
  330.8 5.2 %add_convert_fusion.2 = bf16[1024,768]{1,0:T(8,128)(2,1)} fusion(f32[1024,768]{1,0:T(8,128)S(1)} %copy-done.3, bf16[1024,2304]{0,1:T(8,128)(2,1)S(1)} %bitcast.188, bf16[768,2304]{1,0:T(8,128)(2,1)S(1)} %bitcast.219, f32[1024]{0:T(1024)S(1)} %copy-done.31), kind=kOutput, calls=%fused_computation.86 | convolution fusion | flops 3626237952 | bytes 12980224 | tf_op jit(solution)/shard_map/te,de->td/dot_general | solution.py:532
  336.6 5.6 %convolution_convert_fusion.2 = bf16[2304,768]{0,1:T(8,128)(2,1)} fusion(bf16[1024,2304]{0,1:T(8,128)(2,1)S(1)} %bitcast.190, bf16[1024,768]{1,0:T(8,128)(2,1)S(1)} %copy-done.38), kind=kOutput, calls=%fused_computation.70 | convolution fusion | flops 3625648128 | bytes 9830400 | tf_op jit(solution)/shard_map/td,te->de/dot_general | solution.py:527
  343.4 124.5 %shard_map.280 = (f32[24,2304]{1,0:T(8,128)}, f32[24,768]{1,0:T(8,128)}, f32[24,3072]{1,0:T(8,128)}, f32[96,768]{1,0:T(8,128)}, f32[8,128]{1,0:T(8,128)}) custom-call(bf16[32,24,2304]{2,1,0:T(8,128)(2,1)} %bitcast.195, bf16[32,24,768]{2,1,0:T(8,128)(2,1)} %bitcast.198, bf16[32,24,3072]{2,1,0:T(8,128)(2,1)} %bitcast.194, bf16[32,96,768]{2,1,0:T(8,128)(2,1)} %bitcast.193, ...), custom_call_target="tpu_custom_call" | custom-call | tf_op jit(solution)/shard_map/pallas_call | solution.py:300
  467.9 1.2 slice.74
  469.2 1.6 fusion.65
  470.7 1.6 copy.97
  472.4 1.5 copy.98
  473.9 1.7 copy.99
  475.6 1.7 copy.100
  (176 shorter events, 19.9 us)
Async XLA Ops:
  147.2 5.4 %copy-start.8 = (f32[2,1,12,512,1]{3,2,4,1,0:T(8,128)}, f32[2,1,12,512,1]{3,2,4,1,0:T(8,128)S(1)}, u32[]{:S(2)}) copy-start(f32[2,1,12,512,1]{3,2,4,1,0:T(8,128)S(1)} %get-tuple-element.333) | copy-start | bytes 147460
  147.2 5.4 %copy-start.10 = (s32[2,1,512]{2,1,0:T(1,128)}, s32[2,1,512]{2,1,0:T(1,128)S(1)}, u32[]{:S(2)}) copy-start(s32[2,1,512]{2,1,0:T(1,128)S(1)} %get-tuple-element.383) | copy-start | bytes 12292
  147.2 3.6 copy-start.37
  147.2 3.6 copy-start.39
  147.2 6.5 %slice-start = ((s8[4718592]{0:T(1024)(128)(4,1)}), s8[4194304]{0:T(1024)(128)(4,1)S(1)}, s32[]{:S(2)}) async-start(s8[4718592]{0:T(1024)(128)(4,1)} %bitcast.211), calls=%async_computation | async-start | bytes 8388608
  150.8 1.8 copy-start.5
  150.9 2.9 copy-start.28
  150.9 2.9 copy-start.32
  150.9 2.9 copy-start.34
  150.9 2.9 slice-start.1
  150.9 38.2 %slice-start.2 = ((s8[4718592]{0:T(1024)(128)(4,1)}), s8[4194304]{0:T(1024)(128)(4,1)S(1)}, s32[]{:S(2)}) async-start(s8[4718592]{0:T(1024)(128)(4,1)} %bitcast.215), calls=%async_computation.2 | async-start | bytes 8388608
  152.6 36.5 %copy-start = (f32[1024,768]{1,0:T(8,128)}, f32[1024,768]{1,0:T(8,128)S(1)}, u32[]{:S(2)}) copy-start(f32[1024,768]{1,0:T(8,128)S(1)} %get-tuple-element.223) | copy-start | bytes 9437188
  153.2 0.6 copy-start.25
  153.8 35.3 %copy-start.35 = (f32[768]{0:T(1024)S(1)}, f32[768]{0:T(1024)}, u32[]{:S(2)}) copy-start(f32[768]{0:T(1024)} %reshape.614) | copy-start | bytes 9220
  153.8 35.3 %slice-start.3 = ((s8[4718592]{0:T(1024)(128)(4,1)}), s8[524288]{0:T(1024)(128)(4,1)S(1)}, s32[]{:S(2)}) async-start(s8[4718592]{0:T(1024)(128)(4,1)} %bitcast.215), calls=%async_computation.3 | async-start | bytes 1048576
  189.1 5.5 %copy-start.42 = (bf16[1024,3072]{1,0:T(8,128)(2,1)}, bf16[1024,3072]{1,0:T(8,128)(2,1)S(1)}, u32[]{:S(2)}) copy-start(bf16[1024,3072]{1,0:T(8,128)(2,1)S(1)} %get-tuple-element.206) | copy-start | bytes 18874372
  189.1 6.0 %copy-start.4 = (bf16[1024,768]{1,0:T(8,128)(2,1)S(1)}, bf16[1024,768]{1,0:T(8,128)(2,1)}, u32[]{:S(2)}) copy-start(bf16[1024,768]{1,0:T(8,128)(2,1)} %param.22) | copy-start | bytes 4718596
  189.1 6.0 %copy-start.19 = (f32[768]{0:T(1024)S(1)}, f32[768]{0:T(1024)}, u32[]{:S(2)}) copy-start(f32[768]{0:T(1024)} %reshape.615) | copy-start | bytes 9220
  194.6 3.2 copy-start.29
  197.8 3.7 copy-start.20
  197.8 3.7 copy-start.21
  197.8 3.7 copy-start.22
  197.8 3.7 copy-start.23
  197.8 3.7 copy-start.24
  197.8 3.7 copy-start.27
  197.8 3.7 copy-start.33
  221.0 10.4 %copy-start.1 = (f32[1024,768]{1,0:T(8,128)S(1)}, f32[1024,768]{1,0:T(8,128)}, u32[]{:S(2)}) copy-start(f32[1024,768]{1,0:T(8,128)} %copy-done) | copy-start | bytes 9437188
  221.0 10.4 %copy-start.41 = (bf16[1024,3072]{1,0:T(8,128)(2,1)S(1)}, bf16[1024,3072]{1,0:T(8,128)(2,1)}, u32[]{:S(2)}) copy-start(bf16[1024,3072]{1,0:T(8,128)(2,1)} %get-tuple-element.229) | copy-start | bytes 18874372
  231.4 8.4 %copy-start.26 = (f32[1024]{0:T(1024)S(1)}, f32[1024]{0:T(1024)}, u32[]{:S(2)}) copy-start(f32[1024]{0:T(1024)} %copy-done.25) | copy-start | bytes 12292
  241.3 11.0 %copy-start.2 = (f32[1024,768]{1,0:T(8,128)}, f32[1024,768]{1,0:T(8,128)S(1)}, u32[]{:S(2)}) copy-start(f32[1024,768]{1,0:T(8,128)S(1)} %get-tuple-element.201) | copy-start | bytes 9437188
  249.5 6.9 %copy-start.30 = (f32[1024]{0:T(1024)}, f32[1024]{0:T(1024)S(1)}, u32[]{:S(2)}) copy-start(f32[1024]{0:T(1024)S(1)} %negate_multiply_fusion.1) | copy-start | bytes 12292
  252.3 1.7 copy-start.6
  252.6 3.8 copy-start.7
  253.9 3.1 copy-start.40
  259.9 4.9 %copy-start.9 = (f32[2,1,12,512,1]{3,2,4,1,0:T(8,128)S(1)}, f32[2,1,12,512,1]{3,2,4,1,0:T(8,128)}, u32[]{:S(2)}) copy-start(f32[2,1,12,512,1]{3,2,4,1,0:T(8,128)} %copy-done.8) | copy-start | bytes 147460
  259.9 4.9 %copy-start.11 = (s32[2,1,512]{2,1,0:T(1,128)S(1)}, s32[2,1,512]{2,1,0:T(1,128)}, u32[]{:S(2)}) copy-start(s32[2,1,512]{2,1,0:T(1,128)} %copy-done.10) | copy-start | bytes 12292
  326.4 4.1 copy-start.3
  326.4 4.1 copy-start.31
  326.4 4.4 copy-start.36
  330.8 5.7 %copy-start.38 = (bf16[1024,768]{1,0:T(8,128)(2,1)S(1)}, bf16[1024,768]{1,0:T(8,128)(2,1)}, u32[]{:S(2)}) copy-start(bf16[1024,768]{1,0:T(8,128)(2,1)} %param.20) | copy-start | bytes 4718596
  336.5 5.9 %copy-start.17 = (f32[1,32,24]{2,1,0:T(8,128)S(1)}, f32[1,32,24]{2,1,0:T(8,128)}, u32[]{:S(2)}) copy-start(f32[1,32,24]{2,1,0:T(8,128)} %stack.65) | copy-start | bytes 9220
  336.5 5.9 %copy-start.15 = (f32[1,32,24]{2,1,0:T(8,128)S(1)}, f32[1,32,24]{2,1,0:T(8,128)}, u32[]{:S(2)}) copy-start(f32[1,32,24]{2,1,0:T(8,128)} %stack.66) | copy-start | bytes 9220
  336.5 5.9 %copy-start.16 = (f32[1,32,24]{2,1,0:T(8,128)S(1)}, f32[1,32,24]{2,1,0:T(8,128)}, u32[]{:S(2)}) copy-start(f32[1,32,24]{2,1,0:T(8,128)} %stack.67) | copy-start | bytes 9220
  336.5 5.9 %copy-start.14 = (f32[1,32,24]{2,1,0:T(8,128)S(1)}, f32[1,32,24]{2,1,0:T(8,128)}, u32[]{:S(2)}) copy-start(f32[1,32,24]{2,1,0:T(8,128)} %stack.68) | copy-start | bytes 9220
  336.5 5.9 %copy-start.13 = (f32[1,32,24]{2,1,0:T(8,128)S(1)}, f32[1,32,24]{2,1,0:T(8,128)}, u32[]{:S(2)}) copy-start(f32[1,32,24]{2,1,0:T(8,128)} %stack.69) | copy-start | bytes 9220
  336.5 5.9 %copy-start.12 = (f32[1,32,24]{2,1,0:T(8,128)S(1)}, f32[1,32,24]{2,1,0:T(8,128)}, u32[]{:S(2)}) copy-start(f32[1,32,24]{2,1,0:T(8,128)} %stack.70) | copy-start | bytes 9220
  336.6 6.1 %copy-start.18 = (f32[32,96]{1,0:T(8,128)S(1)}, f32[32,96]{1,0:T(8,128)}, u32[]{:S(2)}) copy-start(f32[32,96]{1,0:T(8,128)} %reshape.607) | copy-start | bytes 36868
